TPU v7x, 32 devices: a whole 2x2x4 slice. The times are simulated.
32 devices in a mesh: vert: 4 (over y, x), feat: 8 (over z, core).
Axes of the slice: x: 2, y: 2, z: 4, core: 2. Of those that a mesh axis runs over, the one named last changes fastest.
Arguments:
- features: bfloat16 [32768, 256], P('vert', 'feat'), may hold values from -6 to 6
- tiles: bfloat16 [256, 16, 128, 128], P('vert'), may hold values from -0.1875 to 0.1875
- tile_cols: int32 [256, 16], P('vert'), may hold values from 0 to 79
- tile_count: int32 [256], P('vert'), may hold values from 1 to 16, as said below
- send_list: int32 [4, 4, 4], P('vert'), may hold values from 0 to 63
- weight: bfloat16 [256, 256], replicated, may hold values from -0.375 to 0.375
- bias: float32 [256], replicated, may hold values from -3 to 3
Outputs:
- node_out: bfloat16 [32768, 256], P(('vert', 'feat'))
Inputs may be any that keep to these rules, and one draw needn't show every extreme that they name: Row block r uses tile places 0 to tile_count[r] - 1; in every draw some row block uses all 16.
All inputs are finite; a program needn't handle non-finite values.
Results may differ from a plain program's by a relative error of at most 0.0044.
Values may be sent and summed in bfloat16 or wider, within the bound.
A program may use at most 128 MiB of HBM per device.

v0:
```python
import functools

import jax
import jax.numpy as jnp
from jax import lax
from jax.experimental import pallas as pl
from jax.experimental.pallas import tpu as pltpu
from jax.sharding import PartitionSpec as P

MESH = pl.DeviceIdType.MESH
GROUP = 4
WINDOW = 16


def flipped(index, mask, count):
    total = 0
    bit = 1
    while bit < count:
        total = total + bit * ((index // bit + mask // bit) % 2)
        bit *= 2
    return total


def exchange_kernel(
    dims, cols_in, count_in, send_in, features, tiles, gathered,
    cols, count, send, table_sem, extended, local, outgoing, landed, hidden, pages,
    load_sem, page_sem, halo_send, halo_recv, full_send, full_recv,
):
    verts, feats, blocks, depth, edge, width, slots, group, window = dims
    per_dest = blocks // feats
    parts = per_dest // group
    chunks = feats * parts
    span = group * edge
    dead = blocks + verts * slots
    vert = lax.axis_index("vert")
    feat = lax.axis_index("feat")

    def dest_of(chunk):
        return flipped(feat, feats - 1 - chunk // parts, feats)

    def page_copy(chunk):
        first = dest_of(chunk) * per_dest + (chunk % parts) * group
        slot = chunk % window
        return pltpu.make_async_copy(
            tiles.at[pl.ds(first, group)], pages.at[slot], page_sem.at[slot]
        )

    local_copy = pltpu.make_async_copy(features, local, load_sem)
    local_copy.start()
    tables = [
        pltpu.make_async_copy(source, target, table_sem.at[at])
        for at, (source, target) in enumerate(((send_in, send), (cols_in, cols), (count_in, count)))
    ]
    for table in tables:
        table.start()
    barrier = pltpu.get_barrier_semaphore()
    for step in range(1, verts):
        pl.semaphore_signal(
            barrier, inc=1, device_id=((vert + step) % verts, feat), device_id_type=MESH
        )
    for step in range(1, feats):
        pl.semaphore_signal(
            barrier, inc=1, device_id=(vert, (feat + step) % feats), device_id_type=MESH
        )
    for chunk in range(window):
        page_copy(chunk).start()
    extended[dead] = jnp.zeros((width, edge), jnp.bfloat16)
    local_copy.wait()
    for table in tables:
        table.wait()
    for block in range(blocks):
        extended[block] = local[:, pl.ds(block * edge, edge)]
    for step in range(verts):
        peer = (vert + step) % verts
        for slot in range(slots):
            outgoing[step, slot] = extended[send[0, peer, slot]]
    pl.semaphore_wait(barrier, verts + feats - 2)
    halos = []
    for step in range(1, verts):
        halo = pltpu.make_async_remote_copy(
            src_ref=outgoing.at[step],
            dst_ref=landed.at[step],
            send_sem=halo_send.at[step],
            recv_sem=halo_recv.at[step],
            device_id=((vert + step) % verts, feat),
            device_id_type=MESH,
        )
        halo.start()
        halos.append(halo)
    extended[pl.ds(blocks + vert * slots, slots)] = outgoing[0]
    for step in range(1, verts):
        halos[step - 1].wait()
        source = (vert + verts - step) % verts
        extended[pl.ds(blocks + source * slots, slots)] = landed[step]

    def outputs_of(chunk):
        at = pl.multiple_of((chunk % parts) * span, edge)
        return (
            hidden.at[chunk // parts, :, pl.ds(at, span)],
            gathered.at[pl.ds(pl.multiple_of(feat * width, width), width), pl.ds(at, span)],
        )

    def full_copy(chunk):
        source, target = outputs_of(chunk)
        return pltpu.make_async_remote_copy(
            src_ref=source,
            dst_ref=target,
            send_sem=full_send.at[chunk],
            recv_sem=full_recv.at[chunk],
            device_id=(vert, dest_of(chunk)),
            device_id_type=MESH,
        )

    def aggregate(chunk, carry):
        page_copy(chunk).wait()
        slot = chunk % window
        first = dest_of(chunk) * per_dest + (chunk % parts) * group
        for row in range(group):
            picked = []
            live = count[first + row]
            for place in range(depth):
                column = jnp.where(place < live, cols[place, first + row], dead)
                picked.append(extended[column])
            page = jnp.concatenate([pages[slot, row, place] for place in range(depth)], axis=1)
            total = lax.dot_general(
                page,
                jnp.concatenate(picked, axis=1),
                (((1,), (1,)), ((), ())),
                preferred_element_type=jnp.float32,
            )
            at = pl.multiple_of((chunk % parts) * span + row * edge, edge)
            hidden[chunk // parts, :, pl.ds(at, edge)] = total.T.astype(jnp.bfloat16)

        @pl.when(chunk + window < chunks)
        def _():
            page_copy(chunk + window).start()

        @pl.when(chunk < chunks - parts)
        def _():
            full_copy(chunk).start()

        return carry

    lax.fori_loop(0, chunks, aggregate, 0)
    gathered[pl.ds(pl.multiple_of(feat * width, width), width), :] = hidden[feats - 1]

    def finish(chunk, carry):
        full_copy(chunk).wait()
        return carry

    lax.fori_loop(0, chunks - parts, finish, 0)


def per_device(features, tiles, tile_cols, tile_count, send_list, weight, bias):
    blocks, depth, edge = tiles.shape[:3]
    width = features.shape[1]
    verts, feats = lax.axis_size("vert"), lax.axis_size("feat")
    slots = send_list.shape[2]
    per_dest = blocks // feats
    group = min(GROUP, per_dest)
    chunks = blocks // group
    window = min(WINDOW, chunks)
    rows = per_dest * edge
    dead = blocks + verts * slots
    dims = (verts, feats, blocks, depth, edge, width, slots, group, window)
    gathered = pl.pallas_call(
        functools.partial(exchange_kernel, dims),
        out_shape=jax.ShapeDtypeStruct((feats * width, rows), jnp.bfloat16),
        in_specs=[
            pl.BlockSpec(memory_space=pltpu.HBM),
            pl.BlockSpec(memory_space=pltpu.HBM),
            pl.BlockSpec(memory_space=pltpu.HBM),
            pl.BlockSpec(memory_space=pltpu.HBM),
            pl.BlockSpec(memory_space=pltpu.HBM),
        ],
        out_specs=pl.BlockSpec(memory_space=pltpu.VMEM),
        scratch_shapes=[
            pltpu.SMEM((depth, blocks), jnp.int32),
            pltpu.SMEM((blocks,), jnp.int32),
            pltpu.SMEM(send_list.shape, jnp.int32),
            pltpu.SemaphoreType.DMA((3,)),
            pltpu.VMEM((dead + 1, width, edge), jnp.bfloat16),
            pltpu.VMEM((width, blocks * edge), jnp.bfloat16),
            pltpu.VMEM((verts, slots, width, edge), jnp.bfloat16),
            pltpu.VMEM((verts, slots, width, edge), jnp.bfloat16),
            pltpu.VMEM((feats, width, rows), jnp.bfloat16),
            pltpu.VMEM((window, group, depth, edge, edge), jnp.bfloat16),
            pltpu.SemaphoreType.DMA,
            pltpu.SemaphoreType.DMA((window,)),
            pltpu.SemaphoreType.DMA((verts,)),
            pltpu.SemaphoreType.DMA((verts,)),
            pltpu.SemaphoreType.DMA((chunks,)),
            pltpu.SemaphoreType.DMA((chunks,)),
        ],
        compiler_params=pltpu.CompilerParams(
            collective_id=0, has_side_effects=True, vmem_limit_bytes=60 * 1024 * 1024
        ),
    )(tile_cols.T, tile_count, send_list, features.T, tiles)
    mixed_rows = lax.dot_general(
        gathered, weight, (((0,), (0,)), ((), ())), preferred_element_type=jnp.float32
    )
    return jnp.maximum(mixed_rows + bias, jnp.float32(0.0)).astype(jnp.bfloat16)


def solution(mesh):
    return jax.shard_map(
        per_device,
        mesh=mesh,
        in_specs=(
            P("vert", "feat"),
            P("vert", None, None, None),
            P("vert", None),
            P("vert"),
            P("vert", None, None),
            P(),
            P(),
        ),
        out_specs=P(("vert", "feat"), None),
        check_vma=False,
    )
```

profile of v0, /device:TPU:0, one launch (start us, length us, event | category | flops | bytes accessed | tf_op | source)
XLA Modules:
  0.0 26.7 jit_solution(3425112026443075101)
XLA Ops:
  0.0 0.0 copy-start
  0.0 0.0 copy-start.1
  0.0 24.5 %shard_map.73 = bf16[256,1024]{1,0:T(8,128)(2,1)} custom-call(s32[16,64]{1,0:T(8,128)} %bitcast.5, s32[64]{0:T(128)} %count_in.1, s32[1,4,4]{2,1,0:T(4,128)} %send_in.1, bf16[32,8192]{1,0:T(8,128)(2,1)} %bitcast.4, bf16[64,16,128,128]{3,2,1,0:T(8,128)(2,1)} %tiles.1), custom_call_target="tpu_custom_call" | custom-call | tf_op jit(solution)/shard_map/pallas_call | solution.py:166
  24.5 0.0 copy-done
  24.5 0.0 copy-done.1
  24.5 2.2 %fusion.1 = bf16[1024,256]{1,0:T(8,128)(2,1)} fusion(bf16[256,1024]{1,0:T(8,128)(2,1)} %shard_map.73, bf16[256,256]{1,0:T(8,128)(2,1)S(1)} %copy-done, f32[256]{0:T(256)S(1)} %copy-done.1), kind=kOutput, calls=%fused_computation.2 | convolution fusion | flops 135004160 | bytes 1180672 | tf_op jit(solution)/shard_map/dot_general | solution.py:199
Async XLA Ops:
  0.0 24.5 %copy-start = (bf16[256,256]{1,0:T(8,128)(2,1)S(1)}, bf16[256,256]{1,0:T(8,128)(2,1)}, u32[]{:S(2)}) copy-start(bf16[256,256]{1,0:T(8,128)(2,1)} %param.12) | copy-start | bytes 393220
  0.0 24.5 %copy-start.1 = (f32[256]{0:T(256)S(1)}, f32[256]{0:T(256)}, u32[]{:S(2)}) copy-start(f32[256]{0:T(256)} %param.13) | copy-start | bytes 3076
where the time goes:
time: 26.9 us; the launch traced here: 26.7 us
  Pallas kernels  24.5 us (91%)
  matrix products  2.19 us (8%)
    pallas_call x1, Pallas kernels, per_device(): pl.pallas_call(functools.partial(exchange_kernel, dims), out_shape=jax.Sh...  24.5 us
    dot_general x1, matrix products, per_device(): lax.dot_general(gathered, weight, (((0,), (0,)), ((), ())), preferred_ele...  2.19 us

commit v1 on v0

v1 whole, which is shorter than its diff:
```python
import functools

import jax
import jax.numpy as jnp
from jax import lax
from jax.experimental import pallas as pl
from jax.experimental.pallas import tpu as pltpu
from jax.sharding import PartitionSpec as P

MESH = pl.DeviceIdType.MESH
GROUP = 4


def visiting_order(chip, chips):
    others = [other for other in range(chips) if other != chip]
    if 0 < chip < chips // 2:
        others.remove(chip + 1)
        others.insert(0, chip + 1)
    elif chip == chips - 1 and chips > 2:
        others[-2:] = others[:-3:-1]
    return others + [chip]


def order_code(chip, chips):
    codes = [
        sum(other * chips**at for at, other in enumerate(visiting_order(one, chips)))
        for one in range(chips)
    ]
    code = codes[0]
    for one in range(1, chips):
        code = jnp.where(chip == one, codes[one], code)
    return code


def exchange_kernel(
    dims, cols_in, count_in, send_in, features, tiles, gathered,
    cols, count, send, table_sem, extended, local, outgoing, landed, hidden, pages,
    load_sem, page_sem, halo_send, halo_recv, full_send, full_recv, above, below,
):
    verts, feats, cores, blocks, depth, edge, width, slots, group = dims
    chips = feats // cores
    per_dest = blocks // feats
    parts = per_dest // group
    span = group * edge
    dead = blocks + verts * slots
    vert = lax.axis_index("vert")
    feat = lax.axis_index("feat")
    chip, core = feat // cores, feat % cores

    def next_code(at, code):
        return jnp.where(at % cores == cores - 1, code // chips, code)

    def dest_of(at, code):
        away = at % cores
        mine = code % chips == chip
        return (code % chips) * cores + (core + away + jnp.where(mine, 1, 0)) % cores

    def page_copy(at, code, part):
        first = dest_of(at, code) * per_dest + part * group
        return pltpu.make_async_copy(
            tiles.at[pl.ds(first, group)], pages.at[at, part], page_sem.at[at, part]
        )

    local_copy = pltpu.make_async_copy(features, local, load_sem)
    local_copy.start()
    tables = [
        pltpu.make_async_copy(source, target, table_sem.at[at])
        for at, (source, target) in enumerate(((send_in, send), (cols_in, cols), (count_in, count)))
    ]
    for table in tables:
        table.start()
    barrier = pltpu.get_barrier_semaphore()
    for step in range(1, verts):
        pl.semaphore_signal(
            barrier, inc=1, device_id=((vert + step) % verts, feat), device_id_type=MESH
        )

    def greet(other):
        pl.semaphore_signal(barrier, inc=1, device_id=(vert, other), device_id_type=MESH)

    for step in range(1, cores):
        greet(chip * cores + (core + step) % cores)

    @pl.when(chip > 0)
    def _():
        for other in range(cores):
            greet((chip - 1) * cores + other)

    @pl.when(chip < chips - 1)
    def _():
        for other in range(cores):
            greet((chip + 1) * cores + other)

    code = order_code(chip, chips)
    walk = code
    for at in range(feats):
        for part in range(parts):
            page_copy(at, walk, part).start()
        walk = next_code(at, walk)
    extended[dead] = jnp.zeros((width, edge), jnp.bfloat16)
    tables[0].wait()
    local_copy.wait()
    for block in range(blocks):
        extended[block] = local[:, block * edge : (block + 1) * edge]
    for step in range(verts):
        peer = (vert + step) % verts
        for slot in range(slots):
            outgoing[step, slot] = extended[send[0, peer, slot]]
    neighbours = jnp.where(chip > 0, 1, 0) + jnp.where(chip < chips - 1, 1, 0)
    pl.semaphore_wait(barrier, verts + cores - 2 + cores * neighbours)
    halos = []
    for step in range(1, verts):
        halos.append(
            pltpu.make_async_remote_copy(
                src_ref=outgoing.at[step],
                dst_ref=landed.at[step],
                send_sem=halo_send.at[step],
                recv_sem=halo_recv.at[step],
                device_id=((vert + step) % verts, feat),
                device_id_type=MESH,
            )
        )
    for halo in halos[::-1]:
        halo.start()

    for far in range(2, chips):

        @pl.when((chip >= 1) & (chip + far - 1 <= chips - 1))
        def _():
            if far > 2:
                pl.semaphore_wait(above.at[far - 1], 1)
            pl.semaphore_signal(
                above.at[far], inc=1, device_id=(vert, feat - cores), device_id_type=MESH
            )

        @pl.when((chip <= chips - 2) & (chip - far + 1 >= 0))
        def _():
            if far > 2:
                pl.semaphore_wait(below.at[far - 1], 1)
            pl.semaphore_signal(
                below.at[far], inc=1, device_id=(vert, feat + cores), device_id_type=MESH
            )

    for table in tables[1:]:
        table.wait()
    extended[pl.ds(blocks + vert * slots, slots)] = outgoing[0]
    for step in range(1, verts):
        halos[step - 1].wait()
        source = (vert + verts - step) % verts
        extended[pl.ds(blocks + source * slots, slots)] = landed[step]

    mine = pl.ds(pl.multiple_of(feat * width, width), width)

    def full_copy(at, code):
        return pltpu.make_async_remote_copy(
            src_ref=hidden.at[at],
            dst_ref=gathered.at[mine],
            send_sem=full_send.at[at],
            recv_sem=full_recv.at[feat],
            device_id=(vert, dest_of(at, code)),
            device_id_type=MESH,
        )

    def aggregate(at, code):
        towards = code % chips
        first = dest_of(at, code) * per_dest
        for part in range(parts):
            page_copy(at, code, part).wait()
        for row in range(per_dest):
            picked = []
            live = count[first + row]
            for place in range(depth):
                column = jnp.where(place < live, cols[place, first + row], dead)
                picked.append(extended[column])
            page = jnp.concatenate(
                [pages[at, row // group, row % group, place] for place in range(depth)], axis=1
            )
            total = lax.dot_general(
                page,
                jnp.concatenate(picked, axis=1),
                (((1,), (1,)), ((), ())),
                preferred_element_type=jnp.float32,
            )
            hidden[at, :, row * edge : (row + 1) * edge] = total.T.astype(jnp.bfloat16)

        @pl.when((at % cores == 0) & (chip == 0) & (towards >= 2))
        def _():
            pl.semaphore_wait(above.at[towards], 1)

        @pl.when((at % cores == 0) & (chip == chips - 1) & (towards <= chips - 3))
        def _():
            pl.semaphore_wait(below.at[chips - 1 - towards], 1)

        @pl.when(at < feats - 1)
        def _():
            full_copy(at, code).start()

        return next_code(at, code)

    lax.fori_loop(0, feats, aggregate, code)
    gathered[mine, :] = hidden[feats - 1]

    def finish(at, code):
        full_copy(at, code).wait_send()
        return next_code(at, code)

    lax.fori_loop(0, feats - 1, finish, code)

    def arrive(step, carry):
        source = (feat + step) % feats
        pltpu.make_async_remote_copy(
            src_ref=hidden.at[0],
            dst_ref=gathered.at[pl.ds(pl.multiple_of(source * width, width), width)],
            send_sem=full_send.at[0],
            recv_sem=full_recv.at[source],
            device_id=(vert, source),
            device_id_type=MESH,
        ).wait_recv()
        return carry

    lax.fori_loop(1, feats, arrive, 0)


def per_device(features, tiles, tile_cols, tile_count, send_list, weight, bias):
    blocks, depth, edge = tiles.shape[:3]
    width = features.shape[1]
    verts, feats = lax.axis_size("vert"), lax.axis_size("feat")
    cores = 2 if feats % 2 == 0 else 1
    slots = send_list.shape[2]
    per_dest = blocks // feats
    group = min(GROUP, per_dest)
    parts = per_dest // group
    rows = per_dest * edge
    dead = blocks + verts * slots
    chips = feats // cores
    dims = (verts, feats, cores, blocks, depth, edge, width, slots, group)
    held = [
        pltpu.VMEM((dead + 1, width, edge), jnp.bfloat16),
        pltpu.VMEM((width, blocks * edge), jnp.bfloat16),
        pltpu.VMEM((verts, slots, width, edge), jnp.bfloat16),
        pltpu.VMEM((verts, slots, width, edge), jnp.bfloat16),
        pltpu.VMEM((feats, width, rows), jnp.bfloat16),
        pltpu.VMEM((feats, parts, group, depth, edge, edge), jnp.bfloat16),
    ]
    gathered = pl.pallas_call(
        functools.partial(exchange_kernel, dims),
        out_shape=jax.ShapeDtypeStruct((feats * width, rows), jnp.bfloat16),
        in_specs=[pl.BlockSpec(memory_space=pltpu.HBM)] * 5,
        out_specs=pl.BlockSpec(memory_space=pltpu.VMEM),
        scratch_shapes=[
            pltpu.SMEM((depth, blocks), jnp.int32),
            pltpu.SMEM((blocks,), jnp.int32),
            pltpu.SMEM(send_list.shape, jnp.int32),
            pltpu.SemaphoreType.DMA((3,)),
            *held,
            pltpu.SemaphoreType.DMA,
            pltpu.SemaphoreType.DMA((feats, parts)),
            pltpu.SemaphoreType.DMA((verts,)),
            pltpu.SemaphoreType.DMA((verts,)),
            pltpu.SemaphoreType.DMA((feats,)),
            pltpu.SemaphoreType.DMA((feats,)),
            pltpu.SemaphoreType.REGULAR((chips + 1,)),
            pltpu.SemaphoreType.REGULAR((chips + 1,)),
        ],
        compiler_params=pltpu.CompilerParams(
            collective_id=0, has_side_effects=True, vmem_limit_bytes=60 * 1024 * 1024
        ),
    )(tile_cols.T, tile_count, send_list, features.T, tiles)
    mixed_rows = lax.dot_general(
        gathered, weight, (((0,), (0,)), ((), ())), preferred_element_type=jnp.float32
    )
    return jnp.maximum(mixed_rows + bias, jnp.float32(0.0)).astype(jnp.bfloat16)


def solution(mesh):
    return jax.shard_map(
        per_device,
        mesh=mesh,
        in_specs=(
            P("vert", "feat"),
            P("vert", None, None, None),
            P("vert", None),
            P("vert"),
            P("vert", None, None),
            P(),
            P(),
        ),
        out_specs=P(("vert", "feat"), None),
        check_vma=False,
    )
```

time: 26.9 us -> 25.5 us (0.948)
  the two profiles are of different devices: /device:TPU:0 before, /device:TPU:25 now
where the time goes in v1:
time: 25.5 us; the launch traced here: 25.3 us
  Pallas kernels  23.1 us (91%)
  matrix products  2.19 us (9%)
    pallas_call x1, Pallas kernels, per_device(): pl.pallas_call(functools.partial(exchange_kernel, dims), out_shape=jax.Sh...  23.1 us
    dot_general x1, matrix products, per_device(): lax.dot_general(gathered, weight, (((0,), (0,)), ((), ())), preferred_ele...  2.19 us

profile of v1, /device:TPU:25, one launch (start us, length us, event | category | flops | bytes accessed | tf_op | source)
XLA Modules:
  0.0 25.3 jit_solution(15226174016431478105)
XLA Ops:
  0.0 0.0 copy-start
  0.0 0.0 copy-start.1
  0.0 23.1 %shard_map.73 = bf16[256,1024]{1,0:T(8,128)(2,1)} custom-call(s32[16,64]{1,0:T(8,128)} %bitcast.5, s32[64]{0:T(128)} %count_in.1, s32[1,4,4]{2,1,0:T(4,128)} %send_in.1, bf16[32,8192]{1,0:T(8,128)(2,1)} %bitcast.4, bf16[64,16,128,128]{3,2,1,0:T(8,128)(2,1)} %tiles.1), custom_call_target="tpu_custom_call" | custom-call | tf_op jit(solution)/shard_map/pallas_call | solution.py:245
  23.1 0.0 copy-done
  23.1 0.0 copy-done.1
  23.1 2.2 %fusion.1 = bf16[1024,256]{1,0:T(8,128)(2,1)} fusion(bf16[256,1024]{1,0:T(8,128)(2,1)} %shard_map.73, bf16[256,256]{1,0:T(8,128)(2,1)S(1)} %copy-done, f32[256]{0:T(256)S(1)} %copy-done.1), kind=kOutput, calls=%fused_computation.2 | convolution fusion | flops 135004160 | bytes 1180672 | tf_op jit(solution)/shard_map/dot_general | solution.py:269
Async XLA Ops:
  0.0 23.1 %copy-start = (bf16[256,256]{1,0:T(8,128)(2,1)S(1)}, bf16[256,256]{1,0:T(8,128)(2,1)}, u32[]{:S(2)}) copy-start(bf16[256,256]{1,0:T(8,128)(2,1)} %param.12) | copy-start | bytes 393220
  0.0 23.1 %copy-start.1 = (f32[256]{0:T(256)S(1)}, f32[256]{0:T(256)}, u32[]{:S(2)}) copy-start(f32[256]{0:T(256)} %param.13) | copy-start | bytes 3076

commit v2 on v1

v2 whole, which is shorter than its diff:
```python
import functools

import jax
import jax.numpy as jnp
from jax import lax
from jax.experimental import pallas as pl
from jax.experimental.pallas import tpu as pltpu
from jax.sharding import PartitionSpec as P

MESH = pl.DeviceIdType.MESH
GROUP = 4


def visiting_order(chip, chips):
    half = chips // 2
    upper = list(range(chips - 1, chip, -1))
    if chip < half or half == 0:
        return list(range(chip - 1, -1, -1)) + upper + [chip]
    far = list(range(half))
    if chip == half:
        far = far[::-1]
    return list(range(chip - 1, half - 1, -1)) + far + upper + [chip]


def order_code(chip, chips):
    codes = [
        sum(other * chips**at for at, other in enumerate(visiting_order(one, chips)))
        for one in range(chips)
    ]
    code = codes[0]
    for one in range(1, chips):
        code = jnp.where(chip == one, codes[one], code)
    return code


def exchange_kernel(
    dims, cols_in, count_in, send_in, features, tiles, weight_in, bias_in, out,
    cols, count, send, table_sem, extended, local, outgoing, landed, hidden, pages,
    gathered, weight, bias, load_sem, page_sem, halo_send, halo_recv, full_send, full_recv,
    above, below,
):
    verts, feats, cores, blocks, depth, edge, width, slots, group = dims
    chips = feats // cores
    per_dest = blocks // feats
    parts = per_dest // group
    span = group * edge
    dead = blocks + verts * slots
    vert = lax.axis_index("vert")
    feat = lax.axis_index("feat")
    chip, core = feat // cores, feat % cores

    def next_code(at, code):
        return jnp.where(at % cores == cores - 1, code // chips, code)

    def dest_of(at, code):
        away = at % cores
        mine = code % chips == chip
        return (code % chips) * cores + (core + away + jnp.where(mine, 1, 0)) % cores

    def page_copy(at, code, part):
        first = dest_of(at, code) * per_dest + part * group
        return pltpu.make_async_copy(
            tiles.at[pl.ds(first, group)], pages.at[at, part], page_sem.at[at, part]
        )

    local_copy = pltpu.make_async_copy(features, local, load_sem)
    local_copy.start()
    sources = (send_in, cols_in, count_in, weight_in, bias_in)
    tables = [
        pltpu.make_async_copy(source, target, table_sem.at[at])
        for at, (source, target) in enumerate(zip(sources, (send, cols, count, weight, bias)))
    ]
    for table in tables[:3]:
        table.start()
    barrier = pltpu.get_barrier_semaphore()
    for step in range(1, verts):
        pl.semaphore_signal(
            barrier, inc=1, device_id=((vert + step) % verts, feat), device_id_type=MESH
        )

    def greet(other):
        pl.semaphore_signal(barrier, inc=1, device_id=(vert, other), device_id_type=MESH)

    for step in range(1, cores):
        greet(chip * cores + (core + step) % cores)

    @pl.when(chip < chips - 1)
    def _():
        for other in range(cores):
            greet((chip + 1) * cores + other)

    code = order_code(chip, chips)
    walk = code
    for at in range(feats):
        for part in range(parts):
            page_copy(at, walk, part).start()
        walk = next_code(at, walk)
    for table in tables[3:]:
        table.start()
    extended[dead] = jnp.zeros((width, edge), jnp.bfloat16)
    tables[0].wait()
    local_copy.wait()
    for block in range(blocks):
        extended[block] = local[:, block * edge : (block + 1) * edge]
    for step in range(verts):
        peer = (vert + step) % verts
        for slot in range(slots):
            outgoing[step, slot] = extended[send[0, peer, slot]]
    pl.semaphore_wait(barrier, verts + cores - 2 + cores * jnp.where(chip > 0, 1, 0))

    def halo(step):
        return pltpu.make_async_remote_copy(
            src_ref=outgoing.at[step],
            dst_ref=landed.at[step],
            send_sem=halo_send.at[step],
            recv_sem=halo_recv.at[step],
            device_id=((vert + step) % verts, feat),
            device_id_type=MESH,
        )

    for peer in range(verts):

        @pl.when(peer != vert)
        def _():
            halo((peer + verts - vert) % verts).start()

    def tell(sem, other):
        pl.semaphore_signal(sem, inc=1, device_id=(vert, other), device_id_type=MESH)

    @pl.when(chip > 0)
    def _():
        tell(above.at[1], feat - cores)

    @pl.when(chip < chips - 1)
    def _():
        pl.semaphore_wait(above.at[1], 1)

    for far in range(2, chips):

        @pl.when((chip >= 1) & (chip + far - 1 <= chips - 1))
        def _():
            if far > 2:
                pl.semaphore_wait(above.at[far - 1], 1)
            tell(above.at[far], feat - cores)

        @pl.when((chip <= chips - 2) & (chip - far + 1 >= 0))
        def _():
            if far > 2:
                pl.semaphore_wait(below.at[far - 1], 1)
            tell(below.at[far], feat + cores)

    for table in tables[1:3]:
        table.wait()
    extended[pl.ds(blocks + vert * slots, slots)] = outgoing[0]
    for step in range(1, verts):
        halo(step).wait()
        source = (vert + verts - step) % verts
        extended[pl.ds(blocks + source * slots, slots)] = landed[step]

    def rows_of(source):
        return pl.ds(pl.multiple_of(source * width, width), width)

    def full_copy(at, code, part):
        return pltpu.make_async_remote_copy(
            src_ref=hidden.at[at, part],
            dst_ref=gathered.at[part, rows_of(feat)],
            send_sem=full_send.at[at, part],
            recv_sem=full_recv.at[feat, part],
            device_id=(vert, dest_of(at, code)),
            device_id_type=MESH,
        )

    def aggregate_row(at, dest, part, row):
        picked = []
        line = dest * per_dest + part * group + row
        live = count[line]
        for place in range(depth):
            column = jnp.where(place < live, cols[place, line], dead)
            picked.append(extended[column])
        page = jnp.concatenate([pages[at, part, row, place] for place in range(depth)], axis=1)
        total = lax.dot_general(
            page,
            jnp.concatenate(picked, axis=1),
            (((1,), (1,)), ((), ())),
            preferred_element_type=jnp.float32,
        )
        return total.T.astype(jnp.bfloat16)

    def aggregate(at, code):
        towards = code % chips
        dest = dest_of(at, code)

        @pl.when((at % cores == 0) & (chip == 0) & (towards >= 2))
        def _():
            pl.semaphore_wait(above.at[towards], 1)

        @pl.when((at % cores == 0) & (chip == chips - 1) & (towards <= chips - 3))
        def _():
            pl.semaphore_wait(below.at[chips - 1 - towards], 1)

        for part in range(parts):
            page_copy(at, code, part).wait()
        for part in range(parts):
            for row in range(group):
                hidden[at, part, :, row * edge : (row + 1) * edge] = aggregate_row(
                    at, dest, part, row
                )
            full_copy(at, code, part).start()
        return next_code(at, code)

    code_end = lax.fori_loop(0, feats - 1, aggregate, code)
    for part in range(parts):
        page_copy(feats - 1, code_end, part).wait()
    for part in range(parts):
        for row in range(group):
            gathered[part, rows_of(feat), row * edge : (row + 1) * edge] = aggregate_row(
                feats - 1, feat, part, row
            )
    for table in tables[3:]:
        table.wait()

    def arrive(part):
        def one(step, carry):
            source = (feat + step) % feats
            pltpu.make_async_remote_copy(
                src_ref=hidden.at[0, part],
                dst_ref=gathered.at[part, rows_of(source)],
                send_sem=full_send.at[0, part],
                recv_sem=full_recv.at[source, part],
                device_id=(vert, source),
                device_id_type=MESH,
            ).wait_recv()
            return carry

        return one

    for part in range(parts):
        lax.fori_loop(1, feats, arrive(part), 0)
        mixed_rows = lax.dot_general(
            gathered[part], weight[...], (((0,), (0,)), ((), ())),
            preferred_element_type=jnp.float32,
        )
        out[part * span : (part + 1) * span, :] = jnp.maximum(
            mixed_rows + bias[...], jnp.float32(0.0)
        ).astype(jnp.bfloat16)

    def finish(at, code):
        for part in range(parts):
            full_copy(at, code, part).wait_send()
        return next_code(at, code)

    lax.fori_loop(0, feats - 1, finish, code)


def per_device(features, tiles, tile_cols, tile_count, send_list, weight, bias):
    blocks, depth, edge = tiles.shape[:3]
    width = features.shape[1]
    verts, feats = lax.axis_size("vert"), lax.axis_size("feat")
    cores = 2 if feats % 2 == 0 else 1
    slots = send_list.shape[2]
    per_dest = blocks // feats
    group = min(GROUP, per_dest)
    parts = per_dest // group
    rows = per_dest * edge
    dead = blocks + verts * slots
    chips = feats // cores
    dims = (verts, feats, cores, blocks, depth, edge, width, slots, group)
    held = [
        pltpu.VMEM((dead + 1, width, edge), jnp.bfloat16),
        pltpu.VMEM((width, blocks * edge), jnp.bfloat16),
        pltpu.VMEM((verts, slots, width, edge), jnp.bfloat16),
        pltpu.VMEM((verts, slots, width, edge), jnp.bfloat16),
        pltpu.VMEM((feats - 1, parts, width, group * edge), jnp.bfloat16),
        pltpu.VMEM((feats, parts, group, depth, edge, edge), jnp.bfloat16),
        pltpu.VMEM((parts, feats * width, group * edge), jnp.bfloat16),
    ]
    return pl.pallas_call(
        functools.partial(exchange_kernel, dims),
        out_shape=pltpu.VMEM((rows, weight.shape[1]), jnp.bfloat16),
        in_specs=[pl.BlockSpec(memory_space=pltpu.HBM)] * 7,
        out_specs=pl.BlockSpec(memory_space=pltpu.VMEM),
        scratch_shapes=[
            pltpu.SMEM((depth, blocks), jnp.int32),
            pltpu.SMEM((blocks,), jnp.int32),
            pltpu.SMEM(send_list.shape, jnp.int32),
            pltpu.SemaphoreType.DMA((5,)),
            *held,
            pltpu.VMEM(weight.shape, jnp.bfloat16),
            pltpu.VMEM(bias.shape, jnp.float32),
            pltpu.SemaphoreType.DMA,
            pltpu.SemaphoreType.DMA((feats, parts)),
            pltpu.SemaphoreType.DMA((verts,)),
            pltpu.SemaphoreType.DMA((verts,)),
            pltpu.SemaphoreType.DMA((feats - 1, parts)),
            pltpu.SemaphoreType.DMA((feats, parts)),
            pltpu.SemaphoreType.REGULAR((chips + 1,)),
            pltpu.SemaphoreType.REGULAR((chips + 1,)),
        ],
        compiler_params=pltpu.CompilerParams(
            collective_id=0, has_side_effects=True, vmem_limit_bytes=60 * 1024 * 1024
        ),
    )(*(pltpu.with_memory_space_constraint(one, pltpu.HBM) for one in (tile_cols.T, tile_count, send_list, features.T, tiles, weight, bias)))


def solution(mesh):
    return jax.shard_map(
        per_device,
        mesh=mesh,
        in_specs=(
            P("vert", "feat"),
            P("vert", None, None, None),
            P("vert", None),
            P("vert"),
            P("vert", None, None),
            P(),
            P(),
        ),
        out_specs=P(("vert", "feat"), None),
        check_vma=False,
    )
```

time: 25.5 us -> 23.6 us (0.925)
  the two profiles are of different devices: /device:TPU:25 before, /device:TPU:1 now
where the time goes in v2:
time: 23.6 us; the launch traced here: 23.4 us
  Pallas kernels  22.6 us (96%)
  local copies, waits for them, and re-layouts  0.8 us (3%)
    pallas_call x1, Pallas kernels, per_device(): pl.pallas_call(functools.partial(exchange_kernel, dims), out_shape=pltpu....  22.6 us
    unnamed x1, local copies, waits for them, and re-layouts  0.8 us

profile of v2, /device:TPU:1, one launch (start us, length us, event | category | flops | bytes accessed | tf_op | source)
XLA Modules:
  0.0 23.4 jit_solution(8072060661778436256)
XLA Ops:
  0.0 22.6 %shard_map.73 = bf16[1024,256]{1,0:T(8,128)(2,1)S(1)} custom-call(s32[16,64]{1,0:T(8,128)} %bitcast.3, s32[64]{0:T(128)} %count_in.1, s32[1,4,4]{2,1,0:T(4,128)} %send_in.1, bf16[32,8192]{1,0:T(8,128)(2,1)} %bitcast.2, bf16[64,16,128,128]{3,2,1,0:T(8,128)(2,1)} %tiles.1, bf16[256,256]{1,0:T(8,128)(2,1)} %weight_in.1, f32[256]{0:T(256)} %bias_in.1), custom_call_target="tpu_custom_call" | custom-call | tf_op jit(solution)/shard_map/pallas_call | solution.py:277
  22.6 0.8 %copy.9 = bf16[1024,256]{1,0:T(8,128)(2,1)} copy(bf16[1024,256]{1,0:T(8,128)(2,1)S(1)} %shard_map.73) | data formatting | bytes 1048576

commit v3 on v2

--- a/solution.py
+++ b/solution.py
@@ -13,13 +13,11 @@
 
 def visiting_order(chip, chips):
     half = chips // 2
-    upper = list(range(chips - 1, chip, -1))
-    if chip < half or half == 0:
-        return list(range(chip - 1, -1, -1)) + upper + [chip]
-    far = list(range(half))
-    if chip == half:
-        far = far[::-1]
-    return list(range(chip - 1, half - 1, -1)) + far + upper + [chip]
+    low, high = list(range(half)), list(range(half, chips))
+    if chip < half:
+        return low[:chip][::-1] + high + low[chip + 1 :] + [chip]
+    below, over = high[: chip - half], high[chip - half + 1 :]
+    return low[:-1] + below + low[-1:] + over + [chip]
 
 
 def order_code(chip, chips):
@@ -53,9 +51,8 @@
         return jnp.where(at % cores == cores - 1, code // chips, code)
 
     def dest_of(at, code):
-        away = at % cores
         mine = code % chips == chip
-        return (code % chips) * cores + (core + away + jnp.where(mine, 1, 0)) % cores
+        return (code % chips) * cores + (core + at + jnp.where(mine, 1, 0)) % cores
 
     def page_copy(at, code, part):
         first = dest_of(at, code) * per_dest + part * group
@@ -170,52 +167,68 @@
             device_id_type=MESH,
         )
 
-    def aggregate_row(at, dest, part, row):
-        picked = []
-        line = dest * per_dest + part * group + row
-        live = count[line]
-        for place in range(depth):
-            column = jnp.where(place < live, cols[place, line], dead)
-            picked.append(extended[column])
-        page = jnp.concatenate([pages[at, part, row, place] for place in range(depth)], axis=1)
-        total = lax.dot_general(
-            page,
-            jnp.concatenate(picked, axis=1),
-            (((1,), (1,)), ((), ())),
-            preferred_element_type=jnp.float32,
-        )
-        return total.T.astype(jnp.bfloat16)
-
-    def aggregate(at, code):
+    def products(at, dest, part):
+        totals = []
+        for row in range(group):
+            picked = []
+            line = dest * per_dest + part * group + row
+            live = count[line]
+            for place in range(depth):
+                column = jnp.where(place < live, cols[place, line], dead)
+                picked.append(extended[column])
+            page = jnp.concatenate([pages[at, part, row, place] for place in range(depth)], axis=1)
+            totals.append(
+                lax.dot_general(
+                    page,
+                    jnp.concatenate(picked, axis=1),
+                    (((1,), (1,)), ((), ())),
+                    preferred_element_type=jnp.float32,
+                )
+            )
+        return totals
+
+    def serve(first_at, code, sent):
+        for away in range(cores):
+            for part in range(parts):
+                page_copy(first_at + away, code, part).wait()
+        waiting = None
+
+        def flush(at, part, totals, send_it):
+            for row, total in enumerate(totals):
+                block = total.T.astype(jnp.bfloat16)
+                if send_it:
+                    hidden[at, part, :, row * edge : (row + 1) * edge] = block
+                else:
+                    gathered[part, rows_of(feat), row * edge : (row + 1) * edge] = block
+            if send_it:
+                full_copy(at, code, part).start()
+
+        for away in range(cores):
+            at = first_at + away
+            dest = dest_of(at, code)
+            for part in range(parts):
+                totals = products(at, dest, part)
+                if waiting is not None:
+                    flush(*waiting)
+                waiting = (at, part, totals, away < sent)
+        flush(*waiting)
+
+    def serve_far(step, code):
         towards = code % chips
-        dest = dest_of(at, code)
-
-        @pl.when((at % cores == 0) & (chip == 0) & (towards >= 2))
+
+        @pl.when((chip == 0) & (towards >= 2))
         def _():
             pl.semaphore_wait(above.at[towards], 1)
 
-        @pl.when((at % cores == 0) & (chip == chips - 1) & (towards <= chips - 3))
+        @pl.when((chip == chips - 1) & (towards <= chips - 3))
         def _():
             pl.semaphore_wait(below.at[chips - 1 - towards], 1)
 
-        for part in range(parts):
-            page_copy(at, code, part).wait()
-        for part in range(parts):
-            for row in range(group):
-                hidden[at, part, :, row * edge : (row + 1) * edge] = aggregate_row(
-                    at, dest, part, row
-                )
-            full_copy(at, code, part).start()
-        return next_code(at, code)
-
-    code_end = lax.fori_loop(0, feats - 1, aggregate, code)
-    for part in range(parts):
-        page_copy(feats - 1, code_end, part).wait()
-    for part in range(parts):
-        for row in range(group):
-            gathered[part, rows_of(feat), row * edge : (row + 1) * edge] = aggregate_row(
-                feats - 1, feat, part, row
-            )
+        serve(step * cores, code, cores)
+        return code // chips
+
+    code_end = lax.fori_loop(0, chips - 1, serve_far, code)
+    serve(feats - cores, code_end, cores - 1)
     for table in tables[3:]:
         table.wait()
 

time: 23.6 us -> 21.5 us (0.911)
  the two profiles are of different devices: /device:TPU:1 before, /device:TPU:9 now
where the time goes in v3:
time: 21.5 us; the launch traced here: 21.3 us
  Pallas kernels  20.5 us (95%)
  local copies, waits for them, and re-layouts  0.8 us (4%)
    pallas_call x1, Pallas kernels, per_device(): pl.pallas_call(functools.partial(exchange_kernel, dims), out_shape=pltpu....  20.5 us
    unnamed x1, local copies, waits for them, and re-layouts  0.8 us

profile of v3, /device:TPU:9, one launch (start us, length us, event | category | flops | bytes accessed | tf_op | source)
XLA Modules:
  0.0 21.3 jit_solution(14349808031759327223)
XLA Ops:
  0.0 20.5 %shard_map.73 = bf16[1024,256]{1,0:T(8,128)(2,1)S(1)} custom-call(s32[16,64]{1,0:T(8,128)} %bitcast.3, s32[64]{0:T(128)} %count_in.1, s32[1,4,4]{2,1,0:T(4,128)} %send_in.1, bf16[32,8192]{1,0:T(8,128)(2,1)} %bitcast.2, bf16[64,16,128,128]{3,2,1,0:T(8,128)(2,1)} %tiles.1, bf16[256,256]{1,0:T(8,128)(2,1)} %weight_in.1, f32[256]{0:T(256)} %bias_in.1), custom_call_target="tpu_custom_call" | custom-call | tf_op jit(solution)/shard_map/pallas_call | solution.py:290
  20.5 0.8 %copy.9 = bf16[1024,256]{1,0:T(8,128)(2,1)} copy(bf16[1024,256]{1,0:T(8,128)(2,1)S(1)} %shard_map.73) | data formatting | bytes 1048576

commit v4 on v3

--- a/solution.py
+++ b/solution.py
@@ -9,6 +9,8 @@
 
 MESH = pl.DeviceIdType.MESH
 GROUP = 4
+FINE = 2
+SWAP = (2, 3)
 
 
 def visiting_order(chip, chips):
@@ -157,19 +159,20 @@
     def rows_of(source):
         return pl.ds(pl.multiple_of(source * width, width), width)
 
-    def full_copy(at, code, part):
+    def full_copy(at, code, part, rows):
+        columns = pl.ds(rows[0] * edge, len(rows) * edge)
         return pltpu.make_async_remote_copy(
-            src_ref=hidden.at[at, part],
-            dst_ref=gathered.at[part, rows_of(feat)],
+            src_ref=hidden.at[at, part, :, columns],
+            dst_ref=gathered.at[part, rows_of(feat), columns],
             send_sem=full_send.at[at, part],
             recv_sem=full_recv.at[feat, part],
             device_id=(vert, dest_of(at, code)),
             device_id_type=MESH,
         )
 
-    def products(at, dest, part):
+    def products(at, dest, part, rows):
         totals = []
-        for row in range(group):
+        for row in rows:
             picked = []
             line = dest * per_dest + part * group + row
             live = count[line]
@@ -177,40 +180,42 @@
                 column = jnp.where(place < live, cols[place, line], dead)
                 picked.append(extended[column])
             page = jnp.concatenate([pages[at, part, row, place] for place in range(depth)], axis=1)
-            totals.append(
-                lax.dot_general(
-                    page,
-                    jnp.concatenate(picked, axis=1),
-                    (((1,), (1,)), ((), ())),
-                    preferred_element_type=jnp.float32,
-                )
-            )
+            vectors = jnp.concatenate(picked, axis=1)
+            both = (((1,), (1,)), ((), ()))
+            if row in SWAP:
+                total = lax.dot_general(vectors, page, both, preferred_element_type=jnp.float32)
+            else:
+                total = lax.dot_general(page, vectors, both, preferred_element_type=jnp.float32).T
+            totals.append(total)
         return totals
 
-    def serve(first_at, code, sent):
+    def serve(first_at, code, sent, fine=1):
         for away in range(cores):
             for part in range(parts):
                 page_copy(first_at + away, code, part).wait()
         waiting = None
 
-        def flush(at, part, totals, send_it):
-            for row, total in enumerate(totals):
-                block = total.T.astype(jnp.bfloat16)
+        def flush(at, part, rows, totals, send_it):
+            for row, total in zip(rows, totals):
+                block = total.astype(jnp.bfloat16)
                 if send_it:
                     hidden[at, part, :, row * edge : (row + 1) * edge] = block
                 else:
                     gathered[part, rows_of(feat), row * edge : (row + 1) * edge] = block
             if send_it:
-                full_copy(at, code, part).start()
+                full_copy(at, code, part, rows).start()
 
         for away in range(cores):
             at = first_at + away
             dest = dest_of(at, code)
             for part in range(parts):
-                totals = products(at, dest, part)
-                if waiting is not None:
-                    flush(*waiting)
-                waiting = (at, part, totals, away < sent)
+                pieces = fine if away == 0 and part == 0 else 1
+                for piece in range(pieces):
+                    rows = range(group * piece // pieces, group * (piece + 1) // pieces)
+                    totals = products(at, dest, part, rows)
+                    if waiting is not None:
+                        flush(*waiting)
+                    waiting = (at, part, rows, totals, away < sent)
         flush(*waiting)
 
     def serve_far(step, code):
@@ -224,10 +229,12 @@
         def _():
             pl.semaphore_wait(below.at[chips - 1 - towards], 1)
 
-        serve(step * cores, code, cores)
+        serve(step * cores, code, cores, FINE if isinstance(step, int) else 1)
         return code // chips
 
-    code_end = lax.fori_loop(0, chips - 1, serve_far, code)
+    code_end = code
+    if chips > 1:
+        code_end = lax.fori_loop(1, chips - 1, serve_far, serve_far(0, code))
     serve(feats - cores, code_end, cores - 1)
     for table in tables[3:]:
         table.wait()
@@ -259,7 +266,7 @@
 
     def finish(at, code):
         for part in range(parts):
-            full_copy(at, code, part).wait_send()
+            full_copy(at, code, part, range(group)).wait_send()
         return next_code(at, code)
 
     lax.fori_loop(0, feats - 1, finish, code)

time: 21.5 us -> 21.3 us (level)
  no operation moved by 1% of the time
where the time goes in v4:
time: 21.3 us; the launch traced here: 21.2 us
  Pallas kernels  20.4 us (96%)
  local copies, waits for them, and re-layouts  0.8 us (4%)
    pallas_call x1, Pallas kernels, per_device(): pl.pallas_call(functools.partial(exchange_kernel, dims), out_shape=pltpu....  20.4 us
    unnamed x1, local copies, waits for them, and re-layouts  0.8 us

profile of v4, /device:TPU:9, one launch (start us, length us, event | category | flops | bytes accessed | tf_op | source)
XLA Modules:
  0.0 21.2 jit_solution(8189743984863297873)
XLA Ops:
  0.0 20.4 %shard_map.73 = bf16[1024,256]{1,0:T(8,128)(2,1)S(1)} custom-call(s32[16,64]{1,0:T(8,128)} %bitcast.3, s32[64]{0:T(128)} %count_in.1, s32[1,4,4]{2,1,0:T(4,128)} %send_in.1, bf16[32,8192]{1,0:T(8,128)(2,1)} %bitcast.2, bf16[64,16,128,128]{3,2,1,0:T(8,128)(2,1)} %tiles.1, bf16[256,256]{1,0:T(8,128)(2,1)} %weight_in.1, f32[256]{0:T(256)} %bias_in.1), custom_call_target="tpu_custom_call" | custom-call | tf_op jit(solution)/shard_map/pallas_call | solution.py:297
  20.4 0.8 %copy.9 = bf16[1024,256]{1,0:T(8,128)(2,1)} copy(bf16[1024,256]{1,0:T(8,128)(2,1)S(1)} %shard_map.73) | data formatting | bytes 1048576

commit v5 on v4

--- a/solution.py
+++ b/solution.py
@@ -9,8 +9,7 @@
 
 MESH = pl.DeviceIdType.MESH
 GROUP = 4
-FINE = 2
-SWAP = (2, 3)
+SWAP = (1,)
 
 
 def visiting_order(chip, chips):
@@ -159,13 +158,13 @@
     def rows_of(source):
         return pl.ds(pl.multiple_of(source * width, width), width)
 
-    def full_copy(at, code, part, rows):
-        columns = pl.ds(rows[0] * edge, len(rows) * edge)
+    def full_copy(at, code, first, rows):
+        columns = pl.ds(first * edge, rows * edge)
         return pltpu.make_async_remote_copy(
-            src_ref=hidden.at[at, part, :, columns],
-            dst_ref=gathered.at[part, rows_of(feat), columns],
-            send_sem=full_send.at[at, part],
-            recv_sem=full_recv.at[feat, part],
+            src_ref=hidden.at[at, :, columns],
+            dst_ref=gathered.at[rows_of(feat), columns],
+            send_sem=full_send.at[at],
+            recv_sem=full_recv.at[feat],
             device_id=(vert, dest_of(at, code)),
             device_id_type=MESH,
         )
@@ -189,33 +188,34 @@
             totals.append(total)
         return totals
 
-    def serve(first_at, code, sent, fine=1):
+    def serve(first_at, code, sent, early):
         for away in range(cores):
             for part in range(parts):
                 page_copy(first_at + away, code, part).wait()
         waiting = None
 
-        def flush(at, part, rows, totals, send_it):
-            for row, total in zip(rows, totals):
+        def flush(at, first, totals, send_it):
+            for row, total in enumerate(totals):
                 block = total.astype(jnp.bfloat16)
+                columns = slice((first + row) * edge, (first + row + 1) * edge)
                 if send_it:
-                    hidden[at, part, :, row * edge : (row + 1) * edge] = block
+                    hidden[at, :, columns] = block
                 else:
-                    gathered[part, rows_of(feat), row * edge : (row + 1) * edge] = block
-            if send_it:
-                full_copy(at, code, part, rows).start()
+                    gathered[rows_of(feat), columns] = block
+            done = first + len(totals)
+            if send_it and early:
+                full_copy(at, code, first, len(totals)).start()
+            elif send_it and done == per_dest:
+                full_copy(at, code, 0, per_dest).start()
 
         for away in range(cores):
             at = first_at + away
             dest = dest_of(at, code)
             for part in range(parts):
-                pieces = fine if away == 0 and part == 0 else 1
-                for piece in range(pieces):
-                    rows = range(group * piece // pieces, group * (piece + 1) // pieces)
-                    totals = products(at, dest, part, rows)
-                    if waiting is not None:
-                        flush(*waiting)
-                    waiting = (at, part, rows, totals, away < sent)
+                totals = products(at, dest, part, range(group))
+                if waiting is not None:
+                    flush(*waiting)
+                waiting = (at, part * group, totals, away < sent)
         flush(*waiting)
 
     def serve_far(step, code):
@@ -229,44 +229,41 @@
         def _():
             pl.semaphore_wait(below.at[chips - 1 - towards], 1)
 
-        serve(step * cores, code, cores, FINE if isinstance(step, int) else 1)
+        serve(step * cores, code, cores, isinstance(step, int))
         return code // chips
 
     code_end = code
     if chips > 1:
         code_end = lax.fori_loop(1, chips - 1, serve_far, serve_far(0, code))
-    serve(feats - cores, code_end, cores - 1)
+    serve(feats - cores, code_end, cores - 1, False)
     for table in tables[3:]:
         table.wait()
 
-    def arrive(part):
-        def one(step, carry):
-            source = (feat + step) % feats
-            pltpu.make_async_remote_copy(
-                src_ref=hidden.at[0, part],
-                dst_ref=gathered.at[part, rows_of(source)],
-                send_sem=full_send.at[0, part],
-                recv_sem=full_recv.at[source, part],
-                device_id=(vert, source),
-                device_id_type=MESH,
-            ).wait_recv()
-            return carry
-
-        return one
-
+    def arrive(step, carry):
+        source = (feat + step) % feats
+        pltpu.make_async_remote_copy(
+            src_ref=hidden.at[0],
+            dst_ref=gathered.at[rows_of(source)],
+            send_sem=full_send.at[0],
+            recv_sem=full_recv.at[source],
+            device_id=(vert, source),
+            device_id_type=MESH,
+        ).wait_recv()
+        return carry
+
+    lax.fori_loop(1, feats, arrive, 0)
     for part in range(parts):
-        lax.fori_loop(1, feats, arrive(part), 0)
+        columns = slice(part * span, (part + 1) * span)
         mixed_rows = lax.dot_general(
-            gathered[part], weight[...], (((0,), (0,)), ((), ())),
+            gathered[:, columns], weight[...], (((0,), (0,)), ((), ())),
             preferred_element_type=jnp.float32,
         )
-        out[part * span : (part + 1) * span, :] = jnp.maximum(
-            mixed_rows + bias[...], jnp.float32(0.0)
-        ).astype(jnp.bfloat16)
+        out[columns, :] = jnp.maximum(mixed_rows + bias[...], jnp.float32(0.0)).astype(
+            jnp.bfloat16
+        )
 
     def finish(at, code):
-        for part in range(parts):
-            full_copy(at, code, part, range(group)).wait_send()
+        full_copy(at, code, 0, per_dest).wait_send()
         return next_code(at, code)
 
     lax.fori_loop(0, feats - 1, finish, code)
@@ -290,9 +287,9 @@
         pltpu.VMEM((width, blocks * edge), jnp.bfloat16),
         pltpu.VMEM((verts, slots, width, edge), jnp.bfloat16),
         pltpu.VMEM((verts, slots, width, edge), jnp.bfloat16),
-        pltpu.VMEM((feats - 1, parts, width, group * edge), jnp.bfloat16),
+        pltpu.VMEM((feats - 1, width, rows), jnp.bfloat16),
         pltpu.VMEM((feats, parts, group, depth, edge, edge), jnp.bfloat16),
-        pltpu.VMEM((parts, feats * width, group * edge), jnp.bfloat16),
+        pltpu.VMEM((feats * width, rows), jnp.bfloat16),
     ]
     return pl.pallas_call(
         functools.partial(exchange_kernel, dims),
@@ -311,8 +308,8 @@
             pltpu.SemaphoreType.DMA((feats, parts)),
             pltpu.SemaphoreType.DMA((verts,)),
             pltpu.SemaphoreType.DMA((verts,)),
-            pltpu.SemaphoreType.DMA((feats - 1, parts)),
-            pltpu.SemaphoreType.DMA((feats, parts)),
+            pltpu.SemaphoreType.DMA((feats - 1,)),
+            pltpu.SemaphoreType.DMA((feats,)),
             pltpu.SemaphoreType.REGULAR((chips + 1,)),
             pltpu.SemaphoreType.REGULAR((chips + 1,)),
         ],

time: 21.3 us -> 21.2 us (level)
  no operation moved by 1% of the time
where the time goes in v5:
time: 21.2 us; the launch traced here: 21 us
  Pallas kernels  20.2 us (95%)
  local copies, waits for them, and re-layouts  0.8 us (4%)
    pallas_call x1, Pallas kernels, per_device(): pl.pallas_call(functools.partial(exchange_kernel, dims), out_shape=pltpu....  20.2 us
    unnamed x1, local copies, waits for them, and re-layouts  0.8 us

profile of v5, /device:TPU:9, one launch (start us, length us, event | category | flops | bytes accessed | tf_op | source)
XLA Modules:
  0.0 21.0 jit_solution(10058937146740761958)
XLA Ops:
  0.0 20.2 %shard_map.73 = bf16[1024,256]{1,0:T(8,128)(2,1)S(1)} custom-call(s32[16,64]{1,0:T(8,128)} %bitcast.3, s32[64]{0:T(128)} %count_in.1, s32[1,4,4]{2,1,0:T(4,128)} %send_in.1, bf16[32,8192]{1,0:T(8,128)(2,1)} %bitcast.2, bf16[64,16,128,128]{3,2,1,0:T(8,128)(2,1)} %tiles.1, bf16[256,256]{1,0:T(8,128)(2,1)} %weight_in.1, f32[256]{0:T(256)} %bias_in.1), custom_call_target="tpu_custom_call" | custom-call | tf_op jit(solution)/shard_map/pallas_call | solution.py:294
  20.2 0.8 %copy.9 = bf16[1024,256]{1,0:T(8,128)(2,1)} copy(bf16[1024,256]{1,0:T(8,128)(2,1)S(1)} %shard_map.73) | data formatting | bytes 1048576

commit v6 on v5

--- a/solution.py
+++ b/solution.py
@@ -18,7 +18,7 @@
     if chip < half:
         return low[:chip][::-1] + high + low[chip + 1 :] + [chip]
     below, over = high[: chip - half], high[chip - half + 1 :]
-    return low[:-1] + below + low[-1:] + over + [chip]
+    return low[:-1] + below + over + low[-1:] + [chip]
 
 
 def order_code(chip, chips):

time: 21.2 us -> 21.2 us (level)
  no operation moved by 1% of the time
where the time goes in v6:
time: 21.2 us; the launch traced here: 21 us
  Pallas kernels  20.2 us (95%)
  local copies, waits for them, and re-layouts  0.8 us (4%)
    pallas_call x1, Pallas kernels, per_device(): pl.pallas_call(functools.partial(exchange_kernel, dims), out_shape=pltpu....  20.2 us
    unnamed x1, local copies, waits for them, and re-layouts  0.8 us

profile of v6, /device:TPU:9, one launch (start us, length us, event | category | flops | bytes accessed | tf_op | source)
XLA Modules:
  0.0 21.0 jit_solution(16385772526481503121)
XLA Ops:
  0.0 20.2 %shard_map.73 = bf16[1024,256]{1,0:T(8,128)(2,1)S(1)} custom-call(s32[16,64]{1,0:T(8,128)} %bitcast.3, s32[64]{0:T(128)} %count_in.1, s32[1,4,4]{2,1,0:T(4,128)} %send_in.1, bf16[32,8192]{1,0:T(8,128)(2,1)} %bitcast.2, bf16[64,16,128,128]{3,2,1,0:T(8,128)(2,1)} %tiles.1, bf16[256,256]{1,0:T(8,128)(2,1)} %weight_in.1, f32[256]{0:T(256)} %bias_in.1), custom_call_target="tpu_custom_call" | custom-call | tf_op jit(solution)/shard_map/pallas_call | solution.py:294
  20.2 0.8 %copy.9 = bf16[1024,256]{1,0:T(8,128)(2,1)} copy(bf16[1024,256]{1,0:T(8,128)(2,1)S(1)} %shard_map.73) | data formatting | bytes 1048576
